TPU v7x, 128 devices: a whole 4x4x4 slice. The times are simulated.
128 devices in a mesh: rows: 4 (over y_lo, core), cols: 32 (over z, y_hi, x).
Axes of the slice: x: 4, y: 4 (y_hi: 2, y_lo: 2; y = y_hi * 2 + y_lo), z: 4, core: 2. Of those that a mesh axis runs over, the one named last changes fastest.
Arguments:
- tracer: float32 [384, 1024, 128], P('rows', 'cols'), may hold values from 0.2 to 1.8
- crowding: float32 [384, 1024, 128], P('rows', 'cols'), may hold values from 0.5 to 2
Outputs:
- potential: float32 [384, 1024, 128], P('rows', 'cols')
- tracer_end: float32 [384, 1024, 128], P('rows', 'cols')
All inputs are finite; a program needn't handle non-finite values.
Results may differ from a plain program's by a relative error of at most 0.00002.
Values sent between devices are 32-bit elements; how exact they have to be, the bound alone decides.
A program may use at most 64 MiB of HBM per device.

v0:
```python
import jax
import jax.numpy as jnp
from jax import lax
from jax.sharding import Mesh
from jax.sharding import PartitionSpec as P

STEPS = 6
COLS = ("cols_0", "cols_1", "cols_2")


def padded_2(value, sides, width):
    for axis, dim in sides:
        size, length = (lax.axis_size(axis), value.shape[dim])
        up = [(i, (i + 1) % size) for i in range(size - 1)]
        down = [(j, i) for i, j in up]
        last = lax.slice_in_dim(value, length - width, length, axis=dim)
        leading = lax.slice_in_dim(value, 0, width, axis=dim)
        before = lax.ppermute(last, axis, up)
        after = lax.ppermute(leading, axis, down)
        value = jnp.concatenate([before, value, after], axis=dim)
    return value


def nothing_yet(value, identity):
    return jnp.broadcast_to(jnp.asarray(identity, value.dtype), value.shape)


def entering(value, axes, combine, identity):
    before = start = nothing_yet(value, identity)
    so_far = value
    for axis in reversed(axes):
        length, place = (lax.axis_size(axis), lax.axis_index(axis))
        pieces = lax.all_gather(so_far, axis)
        inside, so_far = (start, start)
        for k in range(length):
            passed = k < place
            so_far = combine(so_far, pieces[k])
            inside = jnp.where(passed, so_far, inside)
        before = combine(inside, before)
    return before


def strip_edges(values, dims):
    for dim in dims:
        values = lax.slice_in_dim(values, 1, values.shape[dim] - 1, axis=dim)
    return values


def neighbour(values, dim, start, dims):
    others = [other for other in dims if other != dim]
    values = strip_edges(values, others)
    return lax.slice_in_dim(values, start, start + values.shape[dim] - 2, axis=dim)


def one_step(padded, crowding):
    middle = strip_edges(padded, (0, 1))
    lower = [neighbour(padded, dim, 0, (0, 1)) for dim in (0, 1)]
    upper = [neighbour(padded, dim, 2, (0, 1)) for dim in (0, 1)]
    spread = lower[0] + upper[0] + lower[1] + upper[1] - 4.0 * middle
    return middle + 0.1 * spread + 0.2 * middle * (1.0 - middle * crowding)


def body(tracer, crowding):
    padded = padded_2(tracer, (("rows", 0), (COLS, 1)), STEPS)
    wide_crowding = padded_2(crowding, (("rows", 0), (COLS, 1)), STEPS - 1)
    for step in range(STEPS):
        later = one_step(padded, wide_crowding)
        values = later
        margin = STEPS - 1 - step
        place = lax.axis_index("rows") * tracer.shape[0] - margin + jnp.arange(values.shape[0])
        keep_cells = (place >= 0) & (place < tracer.shape[0] * lax.axis_size("rows"))
        values = jnp.where(keep_cells.reshape((-1,) + (1,) * 2), values, 0.0)
        place = lax.axis_index(COLS) * tracer.shape[1] - margin + jnp.arange(values.shape[1])
        keep_cells = (place >= 0) & (place < tracer.shape[1] * lax.axis_size(COLS))
        values = jnp.where(keep_cells.reshape((-1,) + (1,) * 1), values, 0.0)
        later = values
        if step < STEPS - 1:
            wide_crowding = strip_edges(wide_crowding, (0, 1))
        padded = later
    tracer = padded
    here = jnp.cumsum(tracer, axis=1)
    total = lax.slice_in_dim(here, here.shape[1] - 1, here.shape[1], axis=1)

    def add_pair(earlier_total, later_total):
        return earlier_total + later_total

    below = entering(total, COLS, add_pair, jnp.zeros_like(total))
    potential = (here + below) / (tracer.shape[1] * lax.axis_size(COLS))
    return (potential, tracer)


def solution(mesh):
    finer = Mesh(
        mesh.devices.reshape(mesh.shape["rows"], 4, 2, 4), ("rows", "cols_0", "cols_1", "cols_2")
    )
    return jax.shard_map(
        body,
        mesh=finer,
        in_specs=(P("rows", COLS, None), P("rows", COLS, None)),
        out_specs=(P("rows", COLS, None), P("rows", COLS, None)),
        check_vma=False,
    )
```

profile of v0, /device:TPU:26, one launch (start us, length us, event | category | flops | bytes accessed | tf_op | source)
XLA Modules:
  0.0 94.9 jit_solution(12846616888013697041)
XLA Ops:
  0.6 1.0 %fusion.53 = (f32[6,32,128]{2,1,0:T(8,128)S(1)}, f32[6,32,128]{2,1,0:T(8,128)S(1)}) fusion(f32[96,32,128]{2,1,0:T(8,128)} %param.2), kind=kLoop, calls=%fused_computation.104 | loop fusion | bytes 393216 | tf_op jit(solution)/shard_map/slice | solution.py:17
  1.6 1.9 %collective-permute-start = (f32[6,32,128]{2,1,0:T(8,128)S(1)}, f32[6,32,128]{2,1,0:T(8,128)S(1)}, u32[]{:S(2)}, u32[]{:S(2)}) collective-permute-start(f32[6,32,128]{2,1,0:T(8,128)S(1)} %get-tuple-element.13), channel_id=1, source_target_pairs={{0,32},{32,64},{64,96},{1,33},{33,65},{65,97},{2,34},{34,66},{66,9... | collective-permute-start | bytes 294920 | tf_op jit(solution)/shard_map/ppermute | solution.py:18
  3.5 0.0 copy-start.2
  3.5 3.8 %collective-permute-start.1 = (f32[6,32,128]{2,1,0:T(8,128)S(1)}, f32[6,32,128]{2,1,0:T(8,128)S(1)}, u32[]{:S(2)}, u32[]{:S(2)}) collective-permute-start(f32[6,32,128]{2,1,0:T(8,128)S(1)} %get-tuple-element.12), channel_id=1, source_target_pairs={{32,0},{64,32},{96,64},{33,1},{65,33},{97,65},{34,2},{66,34},{98,6... | collective-permute-start | bytes 294920 | tf_op jit(solution)/shard_map/ppermute | solution.py:19
  7.3 0.9 fusion.54
  8.3 1.9 %collective-permute-start.4 = (f32[5,32,128]{2,1,0:T(8,128)S(1)}, f32[5,32,128]{2,1,0:T(8,128)S(1)}, u32[]{:S(2)}, u32[]{:S(2)}) collective-permute-start(f32[5,32,128]{2,1,0:T(8,128)S(1)} %get-tuple-element.15), channel_id=1, source_target_pairs={{0,32},{32,64},{64,96},{1,33},{33,65},{65,97},{2,34},{34,66},{66,9... | collective-permute-start | bytes 245768 | tf_op jit(solution)/shard_map/ppermute | solution.py:18
  10.2 3.6 %collective-permute-start.5 = (f32[5,32,128]{2,1,0:T(8,128)S(1)}, f32[5,32,128]{2,1,0:T(8,128)S(1)}, u32[]{:S(2)}, u32[]{:S(2)}) collective-permute-start(f32[5,32,128]{2,1,0:T(8,128)S(1)} %get-tuple-element.14), channel_id=1, source_target_pairs={{32,0},{64,32},{96,64},{33,1},{65,33},{97,65},{34,2},{66,34},{98,6... | collective-permute-start | bytes 245768 | tf_op jit(solution)/shard_map/ppermute | solution.py:19
  14.1 0.0 collective-permute-done.4
  14.1 1.5 %constant_dynamic-update-slice_fusion.4 = f32[106,32,128]{2,1,0:T(8,128)S(1)} fusion(f32[106,32,128]{2,1,0:T(8,128)S(1)} %constant_dynamic-update-slice_fusion.5, f32[96,32,128]{2,1,0:T(8,128)} %param.3), kind=kLoop, calls=%fused_computation.88 | loop fusion | bytes 3145728
  15.6 0.3 collective-permute-done.5
  15.9 0.0 collective-permute-done
  15.9 0.0 copy-done.2
  15.9 0.1 constant_dynamic-update-slice_fusion.1
  16.0 0.0 collective-permute-done.1
  16.1 0.1 fusion.51
  16.1 3.4 %collective-permute-start.2 = (f32[108,6,128]{2,1,0:T(8,128)S(1)}, f32[108,6,128]{2,1,0:T(8,128)S(1)}, u32[]{:S(2)}, u32[]{:S(2)}) collective-permute-start(f32[108,6,128]{2,1,0:T(8,128)S(1)} %get-tuple-element.8), channel_id=1, source_target_pairs={{0,1},{1,2},{2,3},{3,4},{4,5},{5,6},{6,7},{7,8},{8,9},{9,10},{10,1... | collective-permute-start | bytes 995336 | tf_op jit(solution)/shard_map/ppermute | solution.py:18
  19.5 2.4 %collective-permute-start.3 = (f32[108,6,128]{2,1,0:T(8,128)S(1)}, f32[108,6,128]{2,1,0:T(8,128)S(1)}, u32[]{:S(2)}, u32[]{:S(2)}) collective-permute-start(f32[108,6,128]{2,1,0:T(8,128)S(1)} %get-tuple-element.9), channel_id=1, source_target_pairs={{1,0},{2,1},{3,2},{4,3},{5,4},{6,5},{7,6},{8,7},{9,8},{10,9},{11,1... | collective-permute-start | bytes 995336 | tf_op jit(solution)/shard_map/ppermute | solution.py:19
  22.0 0.1 fusion.52
  22.1 3.4 %collective-permute-start.6 = (f32[106,5,128]{2,1,0:T(8,128)S(1)}, f32[106,5,128]{2,1,0:T(8,128)S(1)}, u32[]{:S(2)}, u32[]{:S(2)}) collective-permute-start(f32[106,5,128]{2,1,0:T(8,128)S(1)} %get-tuple-element.10), channel_id=1, source_target_pairs={{0,1},{1,2},{2,3},{3,4},{4,5},{5,6},{6,7},{7,8},{8,9},{9,10},{10,1... | collective-permute-start | bytes 814088 | tf_op jit(solution)/shard_map/ppermute | solution.py:18
  25.5 4.6 %collective-permute-start.7 = (f32[106,5,128]{2,1,0:T(8,128)S(1)}, f32[106,5,128]{2,1,0:T(8,128)S(1)}, u32[]{:S(2)}, u32[]{:S(2)}) collective-permute-start(f32[106,5,128]{2,1,0:T(8,128)S(1)} %get-tuple-element.11), channel_id=1, source_target_pairs={{1,0},{2,1},{3,2},{4,3},{5,4},{6,5},{7,6},{8,7},{9,8},{10,9},{11,1... | collective-permute-start | bytes 814088 | tf_op jit(solution)/shard_map/ppermute | solution.py:19
  30.1 0.3 collective-permute-done.2
  30.3 4.1 %collective-permute-done.3 = f32[108,6,128]{2,1,0:T(8,128)S(1)} collective-permute-done((f32[108,6,128]{2,1,0:T(8,128)S(1)}, f32[108,6,128]{2,1,0:T(8,128)S(1)}, u32[]{:S(2)}, u32[]{:S(2)}) %collective-permute-start.3) | collective-permute-done | bytes 331808 | tf_op jit(solution)/shard_map/ppermute | solution.py:19
  34.5 0.4 pad_maximum_fusion
  34.9 3.0 %collective-permute-done.6 = f32[106,5,128]{2,1,0:T(8,128)S(1)} collective-permute-done((f32[106,5,128]{2,1,0:T(8,128)S(1)}, f32[106,5,128]{2,1,0:T(8,128)S(1)}, u32[]{:S(2)}, u32[]{:S(2)}) %collective-permute-start.6) | collective-permute-done | bytes 271392 | tf_op jit(solution)/shard_map/ppermute | solution.py:18
  37.9 3.1 %collective-permute-done.7 = f32[106,5,128]{2,1,0:T(8,128)S(1)} collective-permute-done((f32[106,5,128]{2,1,0:T(8,128)S(1)}, f32[106,5,128]{2,1,0:T(8,128)S(1)}, u32[]{:S(2)}, u32[]{:S(2)}) %collective-permute-start.7) | collective-permute-done | bytes 271392 | tf_op jit(solution)/shard_map/ppermute | solution.py:19
  41.1 2.8 %fusion.5 = (f32[106,42,128]{2,1,0:T(8,128)S(1)}, f32[106,42,128]{2,1,0:T(8,128)S(1)}) fusion(f32[108,44,128]{2,1,0:T(8,128)S(1)} %pad_maximum_fusion, pred[106]{0:T(512)(128)(4,1)S(1)} %compare_and_fusion, pred[42]{0:T(512)(128)(4,1)S(1)} %compare_and_fusion.1, f32[106,5,128]{2,1,0:T(8,128)S(1)} %collective-permute-done.7, ...), kind=kLoop, calls=%fused_computation.7 | loop fusion | flops 9117696 | bytes 18235540 | tf_op jit(solution)/shard_map/jit(_where)/select_n | solution.py:75
  43.9 2.2 %fusion.10 = f32[104,40,128]{2,1,0:T(8,128)S(1)} fusion(f32[106,42,128]{2,1,0:T(8,128)S(1)} %get-tuple-element.7, f32[106,42,128]{2,1,0:T(8,128)S(1)} %get-tuple-element.6, pred[104]{0:T(512)(128)(4,1)S(1)} %compare_and_fusion.2, pred[40]{0:T(512)(128)(4,1)S(1)} %compare_and_fusion.3), kind=kLoop, calls=%fused_computation.16 | loop fusion | flops 7454720 | bytes 14909584 | tf_op jit(solution)/shard_map/jit(_where)/select_n | solution.py:75
  46.1 2.2 %fusion.18 = f32[102,38,128]{2,1,0:T(8,128)S(1)} fusion(f32[106,42,128]{2,1,0:T(8,128)S(1)} %get-tuple-element.7, f32[104,40,128]{2,1,0:T(8,128)S(1)} %fusion.10, pred[102]{0:T(512)(128)(4,1)S(1)} %compare_and_fusion.4, pred[38]{0:T(512)(128)(4,1)S(1)} %compare_and_fusion.5), kind=kLoop, calls=%fused_computation.28 | loop fusion | flops 6945792 | bytes 13891724 | tf_op jit(solution)/shard_map/jit(_where)/select_n | solution.py:75
  48.3 2.2 %fusion.26 = f32[100,36,128]{2,1,0:T(8,128)S(1)} fusion(f32[106,42,128]{2,1,0:T(8,128)S(1)} %get-tuple-element.7, f32[102,38,128]{2,1,0:T(8,128)S(1)} %fusion.18, pred[100]{0:T(512)(128)(4,1)S(1)} %compare_and_fusion.6, pred[36]{0:T(512)(128)(4,1)S(1)} %compare_and_fusion.7), kind=kLoop, calls=%fused_computation.40 | loop fusion | flops 6451200 | bytes 12902536 | tf_op jit(solution)/shard_map/jit(_where)/select_n | solution.py:75
  50.5 0.0 copy-start
  50.5 2.1 %fusion.34 = f32[98,34,128]{2,1,0:T(8,128)S(1)} fusion(f32[106,42,128]{2,1,0:T(8,128)S(1)} %get-tuple-element.7, f32[100,36,128]{2,1,0:T(8,128)S(1)} %fusion.26, pred[98]{0:T(512)(128)(4,1)S(1)} %compare_and_fusion.8, pred[34]{0:T(512)(128)(4,1)S(1)} %compare_and_fusion.9), kind=kLoop, calls=%fused_computation.52 | loop fusion | flops 5970944 | bytes 11942020 | tf_op jit(solution)/shard_map/jit(_where)/select_n | solution.py:75
  52.7 0.0 copy-done
  52.7 1.6 %fusion.43 = f32[96,32,128]{2,1,0:T(8,128)S(1)} fusion(f32[98,34,128]{2,1,0:T(8,128)S(1)} %fusion.34, f32[96,32,128]{2,1,0:T(8,128)S(1)} %copy-done, pred[96]{0:T(512)(128)(4,1)S(1)} %compare_and_fusion.10, pred[32]{0:T(512)(128)(4,1)S(1)} %compare_and_fusion.11), kind=kLoop, calls=%fused_computation.65 | loop fusion | flops 5505024 | bytes 11010176 | tf_op jit(solution)/shard_map/jit(_where)/select_n | solution.py:75
  54.3 0.0 copy-start.1
  54.3 0.9 fusion.44
  55.2 18.1 %all-gather = f32[384,1,128]{2,0,1:T(8,128)S(1)} all-gather(f32[96,1,128]{2,0,1:T(8,128)S(1)} %slice.330), channel_id=2, replica_groups=mesh['rows'=4,'cols_0'=4,'cols_1'=2,'cols_2'=4] {'cols_2'}, dimensions={0}, use_global_device_ids=true | all-gather | bytes 245760 | tf_op jit(solution)/shard_map/all_gather | solution.py:33
  73.4 6.3 %all_gather.16 = f32[2,96,1,128]{3,1,2,0:T(8,128)S(1)} all-gather(f32[1,96,1,128]{3,1,2,0:T(8,128)S(1)} %fusion.49), channel_id=1, replica_groups=mesh['rows'=4,'cols_0'=4,'cols_1'=2,'cols_2'=4] {'cols_1'}, dimensions={0}, use_global_device_ids=true | all-gather | bytes 147456 | tf_op jit(solution)/shard_map/all_gather | solution.py:33
  79.6 13.0 %all_gather.17 = f32[4,96,1,128]{3,1,2,0:T(8,128)S(1)} all-gather(f32[1,96,1,128]{3,1,2,0:T(8,128)S(1)} %slice_add_fusion.21), channel_id=1, replica_groups=mesh['rows'=4,'cols_0'=4,'cols_1'=2,'cols_2'=4] {'cols_0'}, dimensions={0}, use_global_device_ids=true | all-gather | bytes 245760 | tf_op jit(solution)/shard_map/all_gather | solution.py:33
  92.7 0.0 copy-done.1
  92.7 0.1 add_multiply_fusion
  92.8 2.1 %copy.7 = f32[96,32,128]{2,1,0:T(8,128)} copy(f32[96,32,128]{2,0,1:T(8,128)S(1)} %add_multiply_fusion) | data formatting | bytes 3145728
  (20 shorter events, 0.2 us)
Async XLA Ops:
  1.6 14.3 %collective-permute-start = (f32[6,32,128]{2,1,0:T(8,128)S(1)}, f32[6,32,128]{2,1,0:T(8,128)S(1)}, u32[]{:S(2)}, u32[]{:S(2)}) collective-permute-start(f32[6,32,128]{2,1,0:T(8,128)S(1)} %get-tuple-element.13), channel_id=1, source_target_pairs={{0,32},{32,64},{64,96},{1,33},{33,65},{65,97},{2,34},{34,66},{66,9... | collective-permute-start | bytes 294920 | tf_op jit(solution)/shard_map/ppermute | solution.py:18
  3.5 12.4 %copy-start.2 = (f32[96,32,128]{2,1,0:T(8,128)S(1)}, f32[96,32,128]{2,1,0:T(8,128)}, u32[]{:S(2)}) copy-start(f32[96,32,128]{2,1,0:T(8,128)} %param.2) | copy-start | bytes 4718596
  3.5 12.5 %collective-permute-start.1 = (f32[6,32,128]{2,1,0:T(8,128)S(1)}, f32[6,32,128]{2,1,0:T(8,128)S(1)}, u32[]{:S(2)}, u32[]{:S(2)}) collective-permute-start(f32[6,32,128]{2,1,0:T(8,128)S(1)} %get-tuple-element.12), channel_id=1, source_target_pairs={{32,0},{64,32},{96,64},{33,1},{65,33},{97,65},{34,2},{66,34},{98,6... | collective-permute-start | bytes 294920 | tf_op jit(solution)/shard_map/ppermute | solution.py:19
  8.3 5.8 %collective-permute-start.4 = (f32[5,32,128]{2,1,0:T(8,128)S(1)}, f32[5,32,128]{2,1,0:T(8,128)S(1)}, u32[]{:S(2)}, u32[]{:S(2)}) collective-permute-start(f32[5,32,128]{2,1,0:T(8,128)S(1)} %get-tuple-element.15), channel_id=1, source_target_pairs={{0,32},{32,64},{64,96},{1,33},{33,65},{65,97},{2,34},{34,66},{66,9... | collective-permute-start | bytes 245768 | tf_op jit(solution)/shard_map/ppermute | solution.py:18
  10.2 5.7 %collective-permute-start.5 = (f32[5,32,128]{2,1,0:T(8,128)S(1)}, f32[5,32,128]{2,1,0:T(8,128)S(1)}, u32[]{:S(2)}, u32[]{:S(2)}) collective-permute-start(f32[5,32,128]{2,1,0:T(8,128)S(1)} %get-tuple-element.14), channel_id=1, source_target_pairs={{32,0},{64,32},{96,64},{33,1},{65,33},{97,65},{34,2},{66,34},{98,6... | collective-permute-start | bytes 245768 | tf_op jit(solution)/shard_map/ppermute | solution.py:19
  16.1 14.2 %collective-permute-start.2 = (f32[108,6,128]{2,1,0:T(8,128)S(1)}, f32[108,6,128]{2,1,0:T(8,128)S(1)}, u32[]{:S(2)}, u32[]{:S(2)}) collective-permute-start(f32[108,6,128]{2,1,0:T(8,128)S(1)} %get-tuple-element.8), channel_id=1, source_target_pairs={{0,1},{1,2},{2,3},{3,4},{4,5},{5,6},{6,7},{7,8},{8,9},{9,10},{10,1... | collective-permute-start | bytes 995336 | tf_op jit(solution)/shard_map/ppermute | solution.py:18
  19.5 14.9 %collective-permute-start.3 = (f32[108,6,128]{2,1,0:T(8,128)S(1)}, f32[108,6,128]{2,1,0:T(8,128)S(1)}, u32[]{:S(2)}, u32[]{:S(2)}) collective-permute-start(f32[108,6,128]{2,1,0:T(8,128)S(1)} %get-tuple-element.9), channel_id=1, source_target_pairs={{1,0},{2,1},{3,2},{4,3},{5,4},{6,5},{7,6},{8,7},{9,8},{10,9},{11,1... | collective-permute-start | bytes 995336 | tf_op jit(solution)/shard_map/ppermute | solution.py:19
  22.1 15.9 %collective-permute-start.6 = (f32[106,5,128]{2,1,0:T(8,128)S(1)}, f32[106,5,128]{2,1,0:T(8,128)S(1)}, u32[]{:S(2)}, u32[]{:S(2)}) collective-permute-start(f32[106,5,128]{2,1,0:T(8,128)S(1)} %get-tuple-element.10), channel_id=1, source_target_pairs={{0,1},{1,2},{2,3},{3,4},{4,5},{5,6},{6,7},{7,8},{8,9},{9,10},{10,1... | collective-permute-start | bytes 814088 | tf_op jit(solution)/shard_map/ppermute | solution.py:18
  25.5 15.6 %collective-permute-start.7 = (f32[106,5,128]{2,1,0:T(8,128)S(1)}, f32[106,5,128]{2,1,0:T(8,128)S(1)}, u32[]{:S(2)}, u32[]{:S(2)}) collective-permute-start(f32[106,5,128]{2,1,0:T(8,128)S(1)} %get-tuple-element.11), channel_id=1, source_target_pairs={{1,0},{2,1},{3,2},{4,3},{5,4},{6,5},{7,6},{8,7},{9,8},{10,9},{11,1... | collective-permute-start | bytes 814088 | tf_op jit(solution)/shard_map/ppermute | solution.py:19
  50.5 2.2 %copy-start = (f32[96,32,128]{2,1,0:T(8,128)S(1)}, f32[96,32,128]{2,1,0:T(8,128)}, u32[]{:S(2)}) copy-start(f32[96,32,128]{2,1,0:T(8,128)} %param.3) | copy-start | bytes 4718596
  54.3 38.4 %copy-start.1 = (f32[96,32,128]{2,1,0:T(8,128)}, f32[96,32,128]{2,1,0:T(8,128)S(1)}, u32[]{:S(2)}) copy-start(f32[96,32,128]{2,1,0:T(8,128)S(1)} %fusion.43) | copy-start | bytes 4718596
where the time goes:
time: 95.3 us; the launch traced here: 94.9 us
  blocking collectives  37.4 us (39%)
  starting transfers between devices  25.1 us (26%)
  other arithmetic  14.8 us (16%)
  waiting for transfers between devices  10.9 us (11%)
  local copies, waits for them, and re-layouts  5.78 us (6%)
  between operations  1.01 us (1%)
    all_gather x3, blocking collectives, entering(): pieces = lax.all_gather(so_far, axis)  37.4 us
    ppermute x4, starting transfers between devices, padded_2(): after = lax.ppermute(leading, axis, down)  14.4 us
    select_n x6, other arithmetic, body(): values = jnp.where(keep_cells.reshape((-1,) + (1,) * 1), values, 0.0)  13.1 us
    ppermute x4, starting transfers between devices, padded_2(): before = lax.ppermute(last, axis, up)  10.6 us
    ppermute x4, waiting for transfers between devices, padded_2(): after = lax.ppermute(leading, axis, down)  7.53 us
    unnamed x11, local copies, waits for them, and re-layouts  3.74 us
    ppermute x4, waiting for transfers between devices, padded_2(): before = lax.ppermute(last, axis, up)  3.32 us
  transfers between devices with their start and end apart: 8, of which 5 were waited for; matrix products, arithmetic and copies ran while one was open for 3% of the time, Pallas kernels for 0%

commit v1 on v0

v1 whole, which is shorter than its diff:
```python
import jax
import jax.numpy as jnp
from jax import lax
from jax.experimental import pallas as pl
from jax.experimental.pallas import tpu as pltpu
from jax.sharding import PartitionSpec as P

NY, NX, M = 96, 32, 128
PITCH = 40
Y0 = 8
ROWS = NY + 2 * Y0
DY, DX = 6, 3
QUARTER = NY // 4
MESH = pl.DeviceIdType.MESH
DIRECTIONS = [(dr, dc) for dr in (-1, 0, 1) for dc in (-1, 0, 1) if (dr, dc) != (0, 0)]


def rows_of(dr, depth):
    if dr == 0:
        return (0, NY), (0, NY)
    if dr < 0:
        return (0, depth), (NY, NY + depth)
    return (NY - depth, NY), (-depth, 0)


def window(ref, rows, side, depth):
    low, high = rows
    if side == "all":
        return ref.at[Y0 + low : Y0 + high, 0:NX, :]
    if side == "first":
        return ref.at[Y0 + low : Y0 + high, 0:depth, :]
    if side == "last":
        return ref.at[Y0 + low : Y0 + high, NX - depth : NX, :]
    if side == "right halo":
        return ref.at[Y0 + low : Y0 + high, NX : NX + depth, :]
    return ref.at[Y0 + low - 1 : Y0 + high - 1, PITCH - depth : PITCH, :]


def sides_of(dc):
    if dc == 0:
        return "all", "all"
    if dc < 0:
        return "first", "right halo"
    return "last", "left halo"


def kernel(
    tracer, crowding, end, here, below,
    u, v, w, t3, tot, p1, p2, group, back,
    in_sem, send_t, recv_t, send_w, recv_w, send_x, recv_x,
    send_1, recv_1, send_2, recv_2, send_3, recv_3,
):
    r = lax.axis_index("rows")
    c = lax.axis_index("cols")
    n_r, n_c = 4, 32
    x = lax.rem(c, 4)
    g = lax.div(c, 4)
    load_t = pltpu.make_async_copy(tracer, window(u, (0, NY), "all", 0), in_sem.at[0])
    load_w = pltpu.make_async_copy(crowding, window(w, (0, NY), "all", 0), in_sem.at[1])
    load_t.start()
    load_w.start()

    def exists(dr, dc):
        ok = True
        if dr < 0:
            ok = r > 0
        if dr > 0:
            ok = r < n_r - 1
        if dc < 0:
            ok = ok & (c > 0)
        if dc > 0:
            ok = ok & (c < n_c - 1)
        return ok

    def neighbour(dr, dc):
        return {"rows": r + dr, "cols": c + dc}

    barrier = pltpu.get_barrier_semaphore()
    group_peers = [{"cols": g * 4 + lax.rem(x + o, 4)} for o in (1, 2, 3)]
    line_peers = [{"cols": lax.rem(g + o, 8) * 4 + x} for o in range(1, 8)]
    expected = jnp.int32(len(group_peers) + len(line_peers))
    for peer in group_peers + line_peers:
        pl.semaphore_signal(barrier, inc=1, device_id=peer, device_id_type=MESH)
    for d in DIRECTIONS:
        here_too = exists(*d)
        expected = expected + here_too.astype(jnp.int32)

        @pl.when(here_too)
        def _(d=d):
            pl.semaphore_signal(barrier, inc=1, device_id=neighbour(*d), device_id_type=MESH)

    is_left, is_right, is_top, is_bottom = c == 0, c == n_c - 1, r == 0, r == n_r - 1
    flat = lambda ref: ref.reshape(ROWS * PITCH, M)

    def zero_sides(ref):
        f = flat(ref)
        zero = jnp.zeros((NY + 2 * DY, M), jnp.float32)

        @pl.when(is_left)
        def _():
            f[pl.ds((Y0 - DY) * PITCH - 1, NY + 2 * DY, stride=PITCH), :] = zero

        @pl.when(is_right)
        def _():
            f[pl.ds((Y0 - DY) * PITCH + NX, NY + 2 * DY, stride=PITCH), :] = zero

    def zero_rows(ref, halo):
        f = flat(ref)
        before, width = (4, PITCH) if halo else (0, NX)
        zero = jnp.zeros((width, M), jnp.float32)

        @pl.when(is_top)
        def _():
            f[pl.ds((Y0 - 1) * PITCH - before, width), :] = zero

        @pl.when(is_bottom)
        def _():
            f[pl.ds((Y0 + NY) * PITCH - before, width), :] = zero

    zero_sides(u)
    zero_sides(t3)

    @pl.when(is_top)
    def _():
        u[Y0 - 1, 0:NX, :] = jnp.zeros((NX, M), jnp.float32)

    @pl.when(is_bottom)
    def _():
        u[Y0 + NY, 0:NX, :] = jnp.zeros((NX, M), jnp.float32)

    load_t.wait()
    load_w.wait()
    pl.semaphore_wait(barrier, expected)

    def halo_copies(ref, dy, dx, send, recv, directions):
        out = []
        for k, (dr, dc) in enumerate(directions):
            source, target = rows_of(dr, dy)
            here_side, there_side = sides_of(dc)
            out.append(
                pltpu.make_async_remote_copy(
                    src_ref=window(ref, source, here_side, dx),
                    dst_ref=window(ref, target, there_side, dx),
                    send_sem=send.at[k],
                    recv_sem=recv.at[k],
                    device_id=neighbour(dr, dc),
                    device_id_type=MESH,
                )
            )
        return out

    copies_t = halo_copies(u, DY, DX, send_t, recv_t, DIRECTIONS)
    copies_w = halo_copies(w, DY - 1, DX - 1, send_w, recv_w, DIRECTIONS)
    for copies in (copies_t, copies_w):
        for d, copy in zip(DIRECTIONS, copies):
            pl.when(exists(*d))(copy.start)
    for copies in (copies_t, copies_w):
        for d, copy in zip(DIRECTIONS, copies):
            pl.when(exists(-d[0], -d[1]))(copy.wait_recv)

    fu, fv, fw, f3 = flat(u), flat(v), flat(w), flat(t3)

    def zero_rows_after_arrival(ref):
        zero_rows(ref, True)

    zero_rows_after_arrival(u)

    def step(src, low, high, tiles, store, first=False, last=False):
        def body(i, carry):
            north, centre = carry
            base = pl.multiple_of((Y0 + low + i) * PITCH, 8)
            south, new = [], []
            for k in range(tiles):
                at = base + 8 * k
                s = src[pl.ds(pl.multiple_of(at + PITCH, 8), 8), :]
                left = src[pl.ds(at - 1, 8), :]
                right = src[pl.ds(at + 1, 8), :]
                cr = fw[pl.ds(pl.multiple_of(at, 8), 8), :]
                here_ = centre[k]
                spread = (left + right) + (north[k] + s)
                used = here_ * cr
                if first:
                    used = used + used
                grown = spread + here_ * (8.0 - used)
                new.append(grown * (0.2 if first else 0.05 if last else 0.1))
                south.append(s)
            store(i, base, new)
            return tuple(centre), tuple(south)

        start = (Y0 + low - 1) * PITCH
        north = tuple(src[pl.ds(start + 8 * k, 8), :] for k in range(tiles))
        centre = tuple(src[pl.ds(start + PITCH + 8 * k, 8), :] for k in range(tiles))
        lax.fori_loop(0, high - low, body, (north, centre), unroll=2)

    def store_to(dst):
        def store(i, base, new):
            for k, value in enumerate(new):
                dst[pl.ds(pl.multiple_of(base + 8 * k, 8), 8), :] = value

        return store

    step(fu, -5, NY + 5, 5, store_to(fv), first=True)
    zero_sides(v)
    zero_rows(v, True)
    for d, copy in zip(DIRECTIONS, copies_t):
        pl.when(exists(*d))(copy.wait_send)
    step(fv, -4, NY + 4, 5, store_to(fu))
    zero_sides(u)
    zero_rows(u, True)
    step(fu, -3, NY + 3, 4, store_to(f3))
    zero_rows(t3, False)

    across = [(0, -1), (0, 1)]
    copies_x = []
    for k, (dr, dc) in enumerate(across):
        here_side, there_side = sides_of(dc)
        rows = (-DX, NY + DX)
        copies_x.append(
            pltpu.make_async_remote_copy(
                src_ref=window(t3, rows, here_side, DX),
                dst_ref=window(t3, rows, there_side, DX),
                send_sem=send_x.at[k],
                recv_sem=recv_x.at[k],
                device_id=neighbour(dr, dc),
                device_id_type=MESH,
            )
        )
    for d, copy in zip(across, copies_x):
        pl.when(exists(*d))(copy.start)
    for d, copy in zip(across, copies_x):
        pl.when(exists(-d[0], -d[1]))(copy.wait_recv)

    step(f3, -2, NY + 2, 5, store_to(fv))
    zero_sides(v)
    zero_rows(v, True)
    step(fv, -1, NY + 1, 5, store_to(fu))
    zero_sides(u)
    zero_rows(u, True)

    def store_end(i, base, new):
        for k, value in enumerate(new):
            end[i, 8 * k : 8 * k + 8, :] = value
        total = (new[0] + new[1]) + (new[2] + new[3])
        tot[pl.ds(i, 1), :] = jnp.sum(total, axis=0, keepdims=True)

    step(fu, 0, NY, 4, store_end, last=True)

    copies_1 = []
    for k, (o, peer) in enumerate(zip((1, 2, 3), group_peers)):
        to = lax.rem(x + o, 4)
        copies_1.append(
            pltpu.make_async_remote_copy(
                src_ref=tot.at[pl.ds(pl.multiple_of(to * QUARTER, 8), QUARTER), :],
                dst_ref=p1.at[x],
                send_sem=send_1.at[k],
                recv_sem=recv_1.at[k],
                device_id=peer,
                device_id_type=MESH,
            )
        )
    for copy in copies_1:
        copy.start()
    p1[x] = tot[pl.ds(pl.multiple_of(x * QUARTER, 8), QUARTER), :]

    place = lax.broadcasted_iota(jnp.int32, (8, M), 0)

    def running(i, _):
        carry = jnp.zeros((1, M), jnp.float32)
        for k in range(4):
            value = end[i, 8 * k : 8 * k + 8, :]
            for shift in (1, 2, 4):
                value = value + jnp.where(place >= shift, pltpu.roll(value, shift, 0), 0.0)
            value = value + carry
            here[i, 8 * k : 8 * k + 8, :] = value
            carry = value[7:8, :]
        return 0

    lax.fori_loop(0, NY, running, 0, unroll=2)

    for copy in copies_1:
        copy.wait_recv()
    own = [p1[k] for k in range(4)]
    group[...] = (own[0] + own[1]) + (own[2] + own[3])
    copies_2 = []
    for k, peer in enumerate(line_peers):
        copies_2.append(
            pltpu.make_async_remote_copy(
                src_ref=group,
                dst_ref=p2.at[g],
                send_sem=send_2.at[k],
                recv_sem=recv_2.at[k],
                device_id=peer,
                device_id_type=MESH,
            )
        )
    for copy in copies_2:
        copy.start()
    for copy in copies_2:
        copy.wait_recv()
    before = jnp.zeros((QUARTER, M), jnp.float32)
    for k in range(7):
        before = before + jnp.where(k < g, p2[k], 0.0)
    for k in range(4):
        back[k] = before
        before = before + own[k]
    copies_3 = []
    for k, (o, peer) in enumerate(zip((1, 2, 3), group_peers)):
        to = lax.rem(x + o, 4)
        copies_3.append(
            pltpu.make_async_remote_copy(
                src_ref=back.at[to],
                dst_ref=below.at[pl.ds(pl.multiple_of(x * QUARTER, 8), QUARTER), :],
                send_sem=send_3.at[k],
                recv_sem=recv_3.at[k],
                device_id=peer,
                device_id_type=MESH,
            )
        )
    for copy in copies_3:
        copy.start()
    below[pl.ds(pl.multiple_of(x * QUARTER, 8), QUARTER), :] = back[x]
    for copy in copies_3:
        copy.wait_recv()
    for d, copy in zip(DIRECTIONS, copies_w):
        pl.when(exists(*d))(copy.wait_send)
    for d, copy in zip(across, copies_x):
        pl.when(exists(*d))(copy.wait_send)
    for copy in copies_1 + copies_2 + copies_3:
        copy.wait_send()


def body(tracer, crowding):
    vmem = pl.BlockSpec(memory_space=pltpu.VMEM)
    hbm = pl.BlockSpec(memory_space=pl.ANY)
    f32 = jnp.float32
    dma = pltpu.SemaphoreType.DMA
    end, here, below = pl.pallas_call(
        kernel,
        out_shape=(
            jax.ShapeDtypeStruct((NY, NX, M), f32),
            jax.ShapeDtypeStruct((NY, NX, M), f32),
            jax.ShapeDtypeStruct((NY, M), f32),
        ),
        in_specs=[hbm, hbm],
        out_specs=(vmem, vmem, vmem),
        scratch_shapes=[
            pltpu.VMEM((ROWS, PITCH, M), f32),
            pltpu.VMEM((ROWS, PITCH, M), f32),
            pltpu.VMEM((ROWS, PITCH, M), f32),
            pltpu.VMEM((ROWS, PITCH, M), f32),
            pltpu.VMEM((NY, M), f32),
            pltpu.VMEM((4, QUARTER, M), f32),
            pltpu.VMEM((8, QUARTER, M), f32),
            pltpu.VMEM((QUARTER, M), f32),
            pltpu.VMEM((4, QUARTER, M), f32),
            dma((2,)),
            dma((8,)), dma((8,)), dma((8,)), dma((8,)),
            dma((2,)), dma((2,)),
            dma((3,)), dma((3,)), dma((7,)), dma((7,)), dma((3,)), dma((3,)),
        ],
        compiler_params=pltpu.CompilerParams(
            collective_id=0, has_side_effects=True, vmem_limit_bytes=40 * 1024 * 1024
        ),
    )(tracer, crowding)
    potential = (here + below[:, None, :]) * (1.0 / 1024)
    return (potential, end)


def solution(mesh):
    spec = P("rows", "cols", None)
    return jax.shard_map(body, mesh=mesh, in_specs=(spec, spec), out_specs=(spec, spec), check_vma=False)
```

time: 95.3 us -> 48.7 us (0.51)
  the two profiles are of different devices: /device:TPU:26 before, /device:TPU:0 now
where the time goes in v1:
time: 48.7 us; the launch traced here: 48.6 us
  Pallas kernels  42.6 us (87%)
  local copies, waits for them, and re-layouts  3.95 us (8%)
  other arithmetic  1.39 us (3%)
  between operations  0.65 us (1%)
    pallas_call x1, Pallas kernels, body(): pl.pallas_call(kernel, out_shape=(jax.ShapeDtypeStruct((NY, NX, M), f32),...  42.6 us
    unnamed x5, local copies, waits for them, and re-layouts  3.95 us
    mul x1, other arithmetic, body(): potential = (here + below[:, None, :]) * (1.0 / 1024)  1.39 us

profile of v1, /device:TPU:0, one launch (start us, length us, event | category | flops | bytes accessed | tf_op | source)
XLA Modules:
  0.0 48.6 jit_solution(9870783440464947326)
XLA Ops:
  0.6 0.0 copy-start
  0.6 1.4 %copy-done = f32[96,32,128]{2,1,0:T(8,128)S(1)} copy-done((f32[96,32,128]{2,1,0:T(8,128)S(1)}, f32[96,32,128]{2,1,0:T(8,128)}, u32[]{:S(2)}) %copy-start) | copy-done | bytes 1572888
  2.0 0.0 copy-start.1
  2.0 1.4 %copy-done.1 = f32[96,32,128]{2,1,0:T(8,128)S(1)} copy-done((f32[96,32,128]{2,1,0:T(8,128)S(1)}, f32[96,32,128]{2,1,0:T(8,128)}, u32[]{:S(2)}) %copy-start.1) | copy-done | bytes 1572888
  3.4 42.6 %shard_map.41 = (f32[96,32,128]{2,1,0:T(8,128)S(1)}, f32[96,32,128]{2,1,0:T(8,128)S(1)}, f32[96,128]{1,0:T(8,128)S(1)}) custom-call(f32[96,32,128]{2,1,0:T(8,128)S(1)} %copy-done, f32[96,32,128]{2,1,0:T(8,128)S(1)} %copy-done.1), custom_call_target="tpu_custom_call" | custom-call | tf_op jit(solution)/shard_map/pallas_call | solution.py:337
  46.0 1.4 %add_multiply_fusion = f32[96,32,128]{2,1,0:T(8,128)} fusion(f32[96,32,128]{2,1,0:T(8,128)S(1)} %get-tuple-element.5, f32[96,128]{1,0:T(8,128)S(1)} %get-tuple-element.6), kind=kLoop, calls=%fused_computation | loop fusion | flops 786432 | bytes 3194880 | tf_op jit(solution)/shard_map/mul | solution.py:365
  47.4 1.1 %copy.5 = f32[96,32,128]{2,1,0:T(8,128)} copy(f32[96,32,128]{2,1,0:T(8,128)S(1)} %get-tuple-element.11) | data formatting | bytes 3145728
Async XLA Ops:
  0.6 1.4 %copy-start = (f32[96,32,128]{2,1,0:T(8,128)S(1)}, f32[96,32,128]{2,1,0:T(8,128)}, u32[]{:S(2)}) copy-start(f32[96,32,128]{2,1,0:T(8,128)} %tracer.1) | copy-start | bytes 4718596
  2.0 1.4 %copy-start.1 = (f32[96,32,128]{2,1,0:T(8,128)S(1)}, f32[96,32,128]{2,1,0:T(8,128)}, u32[]{:S(2)}) copy-start(f32[96,32,128]{2,1,0:T(8,128)} %crowding.1) | copy-start | bytes 4718596

commit v2 on v0

v2 whole, which is shorter than its diff:
```python
import jax
import jax.numpy as jnp
from jax import lax
from jax.experimental import pallas as pl
from jax.experimental.pallas import tpu as pltpu
from jax.sharding import PartitionSpec as P

NY, NX, M = 96, 32, 128
PITCH = 40
Y0 = 8
ROWS = NY + 2 * Y0
DY = 6
QUARTER = NY // 4
MESH = pl.DeviceIdType.MESH
DIRECTIONS = [(dr, dc) for dr in (-1, 0, 1) for dc in (-1, 0, 1) if (dr, dc) != (0, 0)]


CHUNKS = 4
A_ENDS = (31, 55, 79, NY + DY)
B_ENDS = (30, 54, 78, NY + DY)
MAIN = (0, 32, 56, 80, NY)
COUNT = 96


def kernel(
    tracer, crowding, end, here, below,
    u, v, w, w_deep, t2, tot, p1, p2, group,
    in_sem, send_sems, recv_sems, chain,
):
    r = lax.axis_index("rows")
    c = lax.axis_index("cols")
    n_r, n_c = 4, 32
    x = lax.rem(c, 4)
    g = lax.div(c, 4)
    z = lax.div(g, 2)
    interior = lambda ref: ref.at[Y0 : Y0 + NY, 0:NX, :]
    load_t = pltpu.make_async_copy(tracer, interior(u), in_sem.at[0])
    load_w = pltpu.make_async_copy(crowding, interior(w), in_sem.at[1])
    load_t.start()
    load_w.start()

    def exists(dr, dc):
        ok = None
        for there in ((r > 0) if dr < 0 else (r < n_r - 1) if dr > 0 else None,
                      (c > 0) if dc < 0 else (c < n_c - 1) if dc > 0 else None):
            if there is not None:
                ok = there if ok is None else ok & there
        return ok

    def neighbour(dr, dc):
        return {"rows": r + dr, "cols": c + dc}

    barrier = pltpu.get_barrier_semaphore()
    group_peers = [{"rows": r, "cols": g * 4 + lax.rem(x + o, 4)} for o in (1, 2, 3)]
    partner = {"rows": r, "cols": (z * 2 + 1 - lax.rem(g, 2)) * 4 + x}
    greeted = [(exists(*d), neighbour(*d)) for d in DIRECTIONS]
    greeted += [(z > 0, {"rows": r, "cols": c - 8}), (z < 3, {"rows": r, "cols": c + 8})]
    expected = jnp.int32(4)
    for peer in group_peers + [partner]:
        pl.semaphore_signal(barrier, inc=1, device_id=peer, device_id_type=MESH)
    for ok, peer in greeted:
        expected = expected + ok.astype(jnp.int32)

        @pl.when(ok)
        def _(peer=peer):
            pl.semaphore_signal(barrier, inc=1, device_id=peer, device_id_type=MESH)

    is_left, is_right, is_top, is_bottom = c == 0, c == n_c - 1, r == 0, r == n_r - 1
    flat = lambda ref: ref.reshape(ROWS * PITCH, M)
    fu, fv, fw, f2 = flat(u), flat(v), flat(w), flat(t2)

    def zero_sides(f, low, high):
        zero = jnp.zeros((high - low, M), jnp.float32)

        @pl.when(is_left)
        def _():
            f[pl.ds((Y0 + low) * PITCH - 1, high - low, stride=PITCH), :] = zero

        @pl.when(is_right)
        def _():
            f[pl.ds((Y0 + low) * PITCH + NX, high - low, stride=PITCH), :] = zero

    def zero_rows(f, low, high, halo=True):
        before, width = (4, PITCH) if halo else (0, NX)
        zero = jnp.zeros((width, M), jnp.float32)
        for edge, row in ((is_top, -1), (is_bottom, NY)):
            if low <= row < high:

                @pl.when(edge)
                def _(row=row):
                    f[pl.ds((Y0 + row) * PITCH - before, width), :] = zero

    zero_sides(fu, -DY, NY + DY)
    zero_sides(f2, -DY, NY + DY)
    zero_rows(fu, -DY, NY + DY)

    sent = []
    used = [0]

    def copy_to(source, target, peer):
        k = used[0]
        used[0] += 1
        return pltpu.make_async_remote_copy(
            src_ref=source, dst_ref=target, send_sem=send_sems.at[k], recv_sem=recv_sems.at[k],
            device_id=peer, device_id_type=MESH,
        )

    def halo(ref, rows, cols, dr, dc):
        (y1, y2), (x1, x2) = rows, cols
        down, aside = -dr * NY, 0
        if dc < 0:
            aside = NX
        if dc > 0:
            down, aside = down - 1, PITCH - NX
        source = ref.at[Y0 + y1 : Y0 + y2, x1:x2, :]
        target = ref.at[Y0 + y1 + down : Y0 + y2 + down, x1 + aside : x2 + aside, :]
        return exists(dr, dc), exists(-dr, -dc), copy_to(source, target, neighbour(dr, dc))

    def when(ok, do):
        if ok is None:
            do()
        else:
            pl.when(ok)(do)

    def start(items):
        for goes, _, copy in items:
            when(goes, copy.start)
            sent.append((goes, copy))

    def arrive(items):
        for _, comes, copy in items:
            when(comes, copy.wait_recv)

    def finish(count=None):
        for goes, copy in sent[:count]:
            when(goes, copy.wait_send)
        del sent[:count]

    load_t.wait()
    load_w.wait()
    pl.semaphore_wait(barrier, expected)

    def edge_cols(dc, low, high):
        return (low, high) if dc < 0 else (NX - high, NX - low)

    def from_row_neighbour(dr):
        t_rows = (0, DY) if dr < 0 else (NY - DY, NY)
        w_rows = (0, DY - 1) if dr < 0 else (NY - DY + 1, NY)
        out = [halo(u, t_rows, (0, NX), dr, 0), halo(w, w_rows, (0, NX), dr, 0)]
        for dc in (-1, 1):
            out.append(halo(u, t_rows, edge_cols(dc, 0, 2), dr, dc))
            out.append(halo(w, w_rows, edge_cols(dc, 0, 3), dr, dc))
        return out

    from_below = from_row_neighbour(-1)
    from_above = from_row_neighbour(1)
    first = []
    for j in range(CHUNKS):
        rows = (MAIN[j], MAIN[j + 1])
        first.append(
            [halo(u, rows, edge_cols(dc, 0, 2), 0, dc) for dc in (-1, 1)]
            + [halo(w, rows, edge_cols(dc, 0, 1), 0, dc) for dc in (-1, 1)]
        )
    deeper = [
        (exists(0, dc), exists(0, -dc), copy_to(
            w.at[Y0 : Y0 + NY, 1:3, :] if dc < 0 else w.at[Y0 : Y0 + NY, NX - 3 : NX - 1, :],
            w_deep.at[Y0 : Y0 + NY, 1:3, :] if dc < 0 else w_deep.at[Y0 - 1 : Y0 + NY - 1, 5:7, :],
            neighbour(0, dc),
        ))
        for dc in (-1, 1)
    ]
    start(from_above)
    start(first[0])
    start(from_below)
    for items in first[1:] + [deeper]:
        start(items)
    first_sends = len(sent)

    @pl.when(z < 3)
    def _():
        pl.semaphore_wait(chain, 1)

    @pl.when(z > 0)
    def _():
        pl.semaphore_signal(chain, inc=1, device_id={"rows": r, "cols": c - 8}, device_id_type=MESH)

    def step(src, low, high, tiles, store, first=False, last=False):
        def body(i, carry):
            north, centre = carry
            base = pl.multiple_of((Y0 + low + i) * PITCH, 8)
            south, new = [], []
            for k in range(tiles):
                at = base + 8 * k
                s = src[pl.ds(pl.multiple_of(at + PITCH, 8), 8), :]
                left = src[pl.ds(at - 1, 8), :]
                right = src[pl.ds(at + 1, 8), :]
                cr = fw[pl.ds(pl.multiple_of(at, 8), 8), :]
                spread = (left + right) + (north[k] + s)
                taken = centre[k] * cr
                if first:
                    taken = taken + taken
                grown = spread + centre[k] * (8.0 - taken)
                new.append(grown * (0.2 if first else 0.05 if last else 0.1))
                south.append(s)
            store(low + i, base, new)
            return tuple(centre), tuple(south)

        at = (Y0 + low - 1) * PITCH
        north = tuple(src[pl.ds(at + 8 * k, 8), :] for k in range(tiles))
        centre = tuple(src[pl.ds(at + PITCH + 8 * k, 8), :] for k in range(tiles))
        lax.fori_loop(0, high - low, body, (north, centre), unroll=2)

    def store_to(dst):
        def store(row, base, new):
            for k, value in enumerate(new):
                dst[pl.ds(pl.multiple_of(base + 8 * k, 8), 8), :] = value

        return store

    def rows_at(ends, j, s):
        return (ends[j - 1] - s if j else s - DY), ends[j] - s

    place = lax.broadcasted_iota(jnp.int32, (8, M), 0)

    second = []
    for j in range(CHUNKS):
        if j == 0:
            arrive(from_above)
        if j == CHUNKS - 1:
            arrive(from_below)
        arrive(first[j])
        low, high = rows_at(A_ENDS, j, 1)
        step(fu, low, high, 5, store_to(fv), first=True)
        zero_sides(fv, low, high)
        zero_rows(fv, low, high)
        low, high = rows_at(A_ENDS, j, 2)
        step(fv, low, high, 4, store_to(f2))
        zero_rows(f2, low, high, False)
        items = [halo(t2, (low, high), edge_cols(dc, 0, 4), 0, dc) for dc in (-1, 1)]
        start(items)
        second.append(items)
    arrive(deeper)
    finish(first_sends)

    def merge(row, low, high):
        mask = (place > low) & (place < high)
        w[row, NX:PITCH, :] = jnp.where(mask, w_deep[row], w[row, NX:PITCH, :])

    def merge_row(i, _):
        merge(i, 0, 7)
        return 0

    merge(Y0 - 1, 4, 7)
    lax.fori_loop(Y0, Y0 + NY - 1, merge_row, 0, unroll=5)
    merge(Y0 + NY - 1, 0, 4)

    def store_end(row, base, new):
        for k, value in enumerate(new):
            end[row, 8 * k : 8 * k + 8, :] = value
        total = (new[0] + new[1]) + (new[2] + new[3])
        tot[pl.ds(row, 1), :] = jnp.sum(total, axis=0, keepdims=True)

    def running(i, _):
        carry = jnp.zeros((1, M), jnp.float32)
        for k in range(4):
            value = end[i, 8 * k : 8 * k + 8, :]
            for shift in (1, 2, 4):
                value = value + jnp.where(place >= shift, pltpu.roll(value, shift, 0), 0.0)
            value = value + carry
            here[i, 8 * k : 8 * k + 8, :] = value
            carry = value[7:8, :]
        return 0

    def quarter(j):
        return pl.ds(j * QUARTER, QUARTER)

    def group_sum(j):
        arrive(totals[j])
        own = [p1[k, quarter(j), :] for k in range(4)]
        group[quarter(j), :] = (own[0] + own[1]) + (own[2] + own[3])
        items = [
            (g + k < 8, g >= k, copy_to(group.at[quarter(j), :], p2.at[g, quarter(j), :], {"rows": r, "cols": c + 4 * k}))
            for k in range(1, 8)
        ]
        start(items)
        return items

    totals, groups = [], []
    for j in range(CHUNKS):
        arrive(second[j])
        low, high = rows_at(B_ENDS, j, 3)
        step(f2, low, high, 5, store_to(fv))
        zero_sides(fv, low, high)
        zero_rows(fv, low, high)
        low, high = rows_at(B_ENDS, j, 4)
        step(fv, low, high, 5, store_to(fu))
        zero_sides(fu, low, high)
        zero_rows(fu, low, high)
        low, high = rows_at(B_ENDS, j, 5)
        step(fu, low, high, 5, store_to(fv))
        zero_sides(fv, low, high)
        zero_rows(fv, low, high)
        low, high = rows_at(B_ENDS, j, 6)
        step(fv, low, high, 4, store_end, last=True)
        items = [(None, None, copy_to(tot.at[quarter(j), :], p1.at[x, quarter(j), :], peer)) for peer in group_peers]
        start(items)
        totals.append(items)
        p1[x, quarter(j), :] = tot[quarter(j), :]
        if j:
            groups.append(group_sum(j - 1))
        lax.fori_loop(low, high, running, 0, unroll=2)
    groups.append(group_sum(CHUNKS - 1))
    for j in range(CHUNKS):
        arrive(groups[j])
        before = jnp.zeros((QUARTER, M), jnp.float32)
        for k in range(7):
            before = before + jnp.where(k < g, p2[k, quarter(j), :], 0.0)
        for k in range(3):
            before = before + jnp.where(k < x, p1[k, quarter(j), :], 0.0)
        below[quarter(j), :] = before
    finish()

def body(tracer, crowding):
    vmem = pl.BlockSpec(memory_space=pltpu.VMEM)
    hbm = pl.BlockSpec(memory_space=pltpu.HBM)
    f32 = jnp.float32
    dma = pltpu.SemaphoreType.DMA
    end, here, below = pl.pallas_call(
        kernel,
        out_shape=(
            jax.ShapeDtypeStruct((NY, NX, M), f32),
            jax.ShapeDtypeStruct((NY, NX, M), f32),
            jax.ShapeDtypeStruct((NY, M), f32),
        ),
        in_specs=[hbm, hbm],
        out_specs=(vmem, vmem, vmem),
        scratch_shapes=[
            pltpu.VMEM((ROWS, PITCH, M), f32),
            pltpu.VMEM((ROWS, PITCH, M), f32),
            pltpu.VMEM((ROWS, PITCH, M), f32),
            pltpu.VMEM((ROWS, 8, M), f32),
            pltpu.VMEM((ROWS, PITCH, M), f32),
            pltpu.VMEM((NY, M), f32),
            pltpu.VMEM((4, NY, M), f32),
            pltpu.VMEM((8, NY, M), f32),
            pltpu.VMEM((NY, M), f32),
            dma((2,)), dma((COUNT,)), dma((COUNT,)),
            pltpu.SemaphoreType.REGULAR,
        ],
        compiler_params=pltpu.CompilerParams(
            collective_id=0, has_side_effects=True, vmem_limit_bytes=50 * 1024 * 1024
        ),
    )(tracer, crowding)
    potential = (here + below[:, None, :]) * (1.0 / 1024)
    return (potential, end)


def solution(mesh):
    spec = P("rows", "cols", None)
    return jax.shard_map(body, mesh=mesh, in_specs=(spec, spec), out_specs=(spec, spec), check_vma=False)
```

time: 95.3 us -> 44.1 us (0.46)
  the two profiles are of different devices: /device:TPU:26 before, /device:TPU:104 now
where the time goes in v2:
time: 44.1 us; the launch traced here: 43.9 us
  Pallas kernels  40.8 us (93%)
  other arithmetic  1.39 us (3%)
  local copies, waits for them, and re-layouts  1.14 us (3%)
  between operations  0.64 us (1%)
    pallas_call x1, Pallas kernels, body(): pl.pallas_call(kernel, out_shape=(jax.ShapeDtypeStruct((NY, NX, M), f32),...  40.8 us
    mul x1, other arithmetic, body(): potential = (here + below[:, None, :]) * (1.0 / 1024)  1.39 us
    unnamed x1, local copies, waits for them, and re-layouts  1.14 us

profile of v2, /device:TPU:104, one launch (start us, length us, event | category | flops | bytes accessed | tf_op | source)
XLA Modules:
  0.0 43.9 jit_solution(2083004733309782071)
XLA Ops:
  0.6 40.8 %shard_map.41 = (f32[96,32,128]{2,1,0:T(8,128)S(1)}, f32[96,32,128]{2,1,0:T(8,128)S(1)}, f32[96,128]{1,0:T(8,128)S(1)}) custom-call(f32[96,32,128]{2,1,0:T(8,128)} %tracer.1, f32[96,32,128]{2,1,0:T(8,128)} %crowding.1), custom_call_target="tpu_custom_call" | custom-call | tf_op jit(solution)/shard_map/pallas_call | solution.py:328
  41.4 1.4 %add_multiply_fusion = f32[96,32,128]{2,1,0:T(8,128)} fusion(f32[96,32,128]{2,1,0:T(8,128)S(1)} %get-tuple-element.5, f32[96,128]{1,0:T(8,128)S(1)} %get-tuple-element.6), kind=kLoop, calls=%fused_computation | loop fusion | flops 786432 | bytes 3194880 | tf_op jit(solution)/shard_map/mul | solution.py:354
  42.8 1.1 %copy.5 = f32[96,32,128]{2,1,0:T(8,128)} copy(f32[96,32,128]{2,1,0:T(8,128)S(1)} %get-tuple-element.11) | data formatting | bytes 3145728

commit v3 on v2

--- a/solution.py
+++ b/solution.py
@@ -1,3 +1,5 @@
+import functools
+
 import jax
 import jax.numpy as jnp
 from jax import lax
@@ -16,9 +18,10 @@
 
 
 CHUNKS = 4
-A_ENDS = (31, 55, 79, NY + DY)
-B_ENDS = (30, 54, 78, NY + DY)
-MAIN = (0, 32, 56, 80, NY)
+CAP = CHUNKS
+A_ENDS = (37, 61, 85, NY + DY)
+B_ENDS = (36, 60, 84, NY + DY)
+MAIN = (0, 38, 62, 86, NY)
 COUNT = 96
 
 
@@ -70,15 +73,15 @@
     fu, fv, fw, f2 = flat(u), flat(v), flat(w), flat(t2)
 
     def zero_sides(f, low, high):
-        zero = jnp.zeros((high - low, M), jnp.float32)
+        zero = jnp.zeros((high + 1 - low, M), jnp.float32)
 
         @pl.when(is_left)
         def _():
-            f[pl.ds((Y0 + low) * PITCH - 1, high - low, stride=PITCH), :] = zero
+            f[pl.ds((Y0 + low) * PITCH - 1, high + 1 - low, stride=PITCH), :] = zero
 
         @pl.when(is_right)
         def _():
-            f[pl.ds((Y0 + low) * PITCH + NX, high - low, stride=PITCH), :] = zero
+            f[pl.ds((Y0 + low) * PITCH + NX, high + 1 - low, stride=PITCH), :] = zero
 
     def zero_rows(f, low, high, halo=True):
         before, width = (4, PITCH) if halo else (0, NX)
@@ -176,13 +179,21 @@
         start(items)
     first_sends = len(sent)
 
-    @pl.when(z < 3)
-    def _():
-        pl.semaphore_wait(chain, 1)
-
-    @pl.when(z > 0)
-    def _():
-        pl.semaphore_signal(chain, inc=1, device_id={"rows": r, "cols": c - 8}, device_id_type=MESH)
+
+    def chain_stage(k):
+        if k > 0:
+
+            @pl.when(z < 3)
+            def _():
+                pl.semaphore_wait(chain.at[k - 1], 1)
+
+        if k < 3:
+
+            @pl.when(z > 0)
+            def _():
+                pl.semaphore_signal(chain.at[k], inc=1, device_id={"rows": r, "cols": c - 8}, device_id_type=MESH)
+
+    chain_stage(0)
 
     def step(src, low, high, tiles, store, first=False, last=False):
         def body(i, carry):
@@ -218,17 +229,20 @@
         return store
 
     def rows_at(ends, j, s):
-        return (ends[j - 1] - s if j else s - DY), ends[j] - s
+        if j == CAP:
+            return s - DY, s
+        return (ends[j - 1] - s if j else s), ends[j] - s
 
     place = lax.broadcasted_iota(jnp.int32, (8, M), 0)
 
     second = []
-    for j in range(CHUNKS):
-        if j == 0:
+    for j in range(CHUNKS + 1):
+        if j == CAP:
             arrive(from_above)
+        else:
+            arrive(first[j])
         if j == CHUNKS - 1:
             arrive(from_below)
-        arrive(first[j])
         low, high = rows_at(A_ENDS, j, 1)
         step(fu, low, high, 5, store_to(fv), first=True)
         zero_sides(fv, low, high)
@@ -239,6 +253,8 @@
         items = [halo(t2, (low, high), edge_cols(dc, 0, 4), 0, dc) for dc in (-1, 1)]
         start(items)
         second.append(items)
+        if j in (0, 2):
+            chain_stage(1 + j // 2)
     arrive(deeper)
     finish(first_sends)
 
@@ -254,11 +270,11 @@
     lax.fori_loop(Y0, Y0 + NY - 1, merge_row, 0, unroll=5)
     merge(Y0 + NY - 1, 0, 4)
 
-    def store_end(row, base, new):
+    def store_end(row, base, new, first_row):
         for k, value in enumerate(new):
             end[row, 8 * k : 8 * k + 8, :] = value
         total = (new[0] + new[1]) + (new[2] + new[3])
-        tot[pl.ds(row, 1), :] = jnp.sum(total, axis=0, keepdims=True)
+        tot[pl.ds(row - DY if first_row >= DY else row + NY - DY, 1), :] = jnp.sum(total, axis=0, keepdims=True)
 
     def running(i, _):
         carry = jnp.zeros((1, M), jnp.float32)
@@ -286,7 +302,7 @@
         return items
 
     totals, groups = [], []
-    for j in range(CHUNKS):
+    for j in range(CHUNKS + 1):
         arrive(second[j])
         low, high = rows_at(B_ENDS, j, 3)
         step(f2, low, high, 5, store_to(fv))
@@ -301,15 +317,18 @@
         zero_sides(fv, low, high)
         zero_rows(fv, low, high)
         low, high = rows_at(B_ENDS, j, 6)
-        step(fv, low, high, 4, store_end, last=True)
-        items = [(None, None, copy_to(tot.at[quarter(j), :], p1.at[x, quarter(j), :], peer)) for peer in group_peers]
+        step(fv, low, high, 4, functools.partial(store_end, first_row=low), last=True)
+        if j == CHUNKS - 1:
+            continue
+        k = min(j, CHUNKS - 1)
+        items = [(None, None, copy_to(tot.at[quarter(k), :], p1.at[x, quarter(k), :], peer)) for peer in group_peers]
         start(items)
         totals.append(items)
-        p1[x, quarter(j), :] = tot[quarter(j), :]
-        if j:
-            groups.append(group_sum(j - 1))
-        lax.fori_loop(low, high, running, 0, unroll=2)
-    groups.append(group_sum(CHUNKS - 1))
+        p1[x, quarter(k), :] = tot[quarter(k), :]
+    chain_stage(3)
+    for j in range(CHUNKS):
+        groups.append(group_sum(j))
+    lax.fori_loop(0, NY, running, 0, unroll=2)
     for j in range(CHUNKS):
         arrive(groups[j])
         before = jnp.zeros((QUARTER, M), jnp.float32)
@@ -317,7 +336,12 @@
             before = before + jnp.where(k < g, p2[k, quarter(j), :], 0.0)
         for k in range(3):
             before = before + jnp.where(k < x, p1[k, quarter(j), :], 0.0)
-        below[quarter(j), :] = before
+        at = DY + j * QUARTER
+        if j < CHUNKS - 1:
+            below[at : at + QUARTER, :] = before
+        else:
+            below[at:NY, :] = before[: NY - at]
+            below[0:DY, :] = before[NY - at :]
     finish()
 
 def body(tracer, crowding):
@@ -345,7 +369,7 @@
             pltpu.VMEM((8, NY, M), f32),
             pltpu.VMEM((NY, M), f32),
             dma((2,)), dma((COUNT,)), dma((COUNT,)),
-            pltpu.SemaphoreType.REGULAR,
+            pltpu.SemaphoreType.REGULAR((3,)),
         ],
         compiler_params=pltpu.CompilerParams(
             collective_id=0, has_side_effects=True, vmem_limit_bytes=50 * 1024 * 1024

time: 44.1 us -> 36.6 us (0.83)
  Pallas kernels: 40.8 us -> 33 us
    pallas_call x1, Pallas kernels: 40.8 us -> 33 us  [body(): pl.pallas_call(kernel, out_shape=(jax.ShapeDtypeStruct((NY, NX, M), f32),...]
where the time goes in v3:
time: 36.6 us; the launch traced here: 36.2 us
  Pallas kernels  33 us (90%)
  other arithmetic  1.39 us (4%)
  local copies, waits for them, and re-layouts  1.14 us (3%)
  between operations  0.64 us (2%)
    pallas_call x1, Pallas kernels, body(): pl.pallas_call(kernel, out_shape=(jax.ShapeDtypeStruct((NY, NX, M), f32),...  33 us
    mul x1, other arithmetic, body(): potential = (here + below[:, None, :]) * (1.0 / 1024)  1.39 us
    unnamed x1, local copies, waits for them, and re-layouts  1.14 us

profile of v3, /device:TPU:104, one launch (start us, length us, event | category | flops | bytes accessed | tf_op | source)
XLA Modules:
  0.0 36.2 jit_solution(2166139694964703353)
XLA Ops:
  0.6 33.0 %shard_map.41 = (f32[96,32,128]{2,1,0:T(8,128)S(1)}, f32[96,32,128]{2,1,0:T(8,128)S(1)}, f32[96,128]{1,0:T(8,128)S(1)}) custom-call(f32[96,32,128]{2,1,0:T(8,128)} %tracer.1, f32[96,32,128]{2,1,0:T(8,128)} %crowding.1), custom_call_target="tpu_custom_call" | custom-call | tf_op jit(solution)/shard_map/pallas_call | solution.py:352
  33.6 1.4 %add_multiply_fusion = f32[96,32,128]{2,1,0:T(8,128)} fusion(f32[96,32,128]{2,1,0:T(8,128)S(1)} %get-tuple-element.5, f32[96,128]{1,0:T(8,128)S(1)} %get-tuple-element.6), kind=kLoop, calls=%fused_computation | loop fusion | flops 786432 | bytes 3194880 | tf_op jit(solution)/shard_map/mul | solution.py:378
  35.0 1.1 %copy.5 = f32[96,32,128]{2,1,0:T(8,128)} copy(f32[96,32,128]{2,1,0:T(8,128)S(1)} %get-tuple-element.11) | data formatting | bytes 3145728

commit v4 on v3

--- a/solution.py
+++ b/solution.py
@@ -19,7 +19,7 @@
 
 CHUNKS = 4
 CAP = CHUNKS
-A_ENDS = (37, 61, 85, NY + DY)
+A_ENDS = (37, 61, 85, NY + 2)
 B_ENDS = (36, 60, 84, NY + DY)
 MAIN = (0, 38, 62, 86, NY)
 COUNT = 96
@@ -83,19 +83,19 @@
         def _():
             f[pl.ds((Y0 + low) * PITCH + NX, high + 1 - low, stride=PITCH), :] = zero
 
-    def zero_rows(f, low, high, halo=True):
-        before, width = (4, PITCH) if halo else (0, NX)
-        zero = jnp.zeros((width, M), jnp.float32)
+    def zero_rows(f, low, high):
+        zero = jnp.zeros((PITCH, M), jnp.float32)
         for edge, row in ((is_top, -1), (is_bottom, NY)):
             if low <= row < high:
 
                 @pl.when(edge)
                 def _(row=row):
-                    f[pl.ds((Y0 + row) * PITCH - before, width), :] = zero
+                    f[pl.ds((Y0 + row) * PITCH - 4, PITCH), :] = zero
 
     zero_sides(fu, -DY, NY + DY)
     zero_sides(f2, -DY, NY + DY)
     zero_rows(fu, -DY, NY + DY)
+    zero_rows(f2, -DY, NY + DY)
 
     sent = []
     used = [0]
@@ -146,14 +146,19 @@
     def edge_cols(dc, low, high):
         return (low, high) if dc < 0 else (NX - high, NX - low)
 
+    def row_halo(ref, low, high, dr, dc, depth=None):
+        rows = (low, high) if dr < 0 else (NY - high, NY - low)
+        return halo(ref, rows, edge_cols(dc, 0, depth) if dc else (0, NX), dr, dc)
+
     def from_row_neighbour(dr):
-        t_rows = (0, DY) if dr < 0 else (NY - DY, NY)
-        w_rows = (0, DY - 1) if dr < 0 else (NY - DY + 1, NY)
-        out = [halo(u, t_rows, (0, NX), dr, 0), halo(w, w_rows, (0, NX), dr, 0)]
+        out = [row_halo(u, 0, 2, dr, 0), row_halo(w, 0, 1, dr, 0)]
         for dc in (-1, 1):
-            out.append(halo(u, t_rows, edge_cols(dc, 0, 2), dr, dc))
-            out.append(halo(w, w_rows, edge_cols(dc, 0, 3), dr, dc))
+            out.append(row_halo(u, 0, 2, dr, dc, 2))
+            out.append(row_halo(w, 0, 3, dr, dc, 3))
         return out
+
+    def again_from_row_neighbour(dr):
+        return [row_halo(t2, 0, 4, dr, dc, 4) for dc in (0, -1, 1)]
 
     from_below = from_row_neighbour(-1)
     from_above = from_row_neighbour(1)
@@ -171,10 +176,10 @@
             neighbour(0, dc),
         ))
         for dc in (-1, 1)
-    ]
+    ] + [row_halo(w, 1, 3, dr, 0) for dr in (-1, 1)]
     start(from_above)
+    start(from_below)
     start(first[0])
-    start(from_below)
     for items in first[1:] + [deeper]:
         start(items)
     first_sends = len(sent)
@@ -230,7 +235,7 @@
 
     def rows_at(ends, j, s):
         if j == CAP:
-            return s - DY, s
+            return s - ends[CHUNKS - 1] + NY, s
         return (ends[j - 1] - s if j else s), ends[j] - s
 
     place = lax.broadcasted_iota(jnp.int32, (8, M), 0)
@@ -249,10 +254,15 @@
         zero_rows(fv, low, high)
         low, high = rows_at(A_ENDS, j, 2)
         step(fv, low, high, 4, store_to(f2))
-        zero_rows(f2, low, high, False)
         items = [halo(t2, (low, high), edge_cols(dc, 0, 4), 0, dc) for dc in (-1, 1)]
         start(items)
         second.append(items)
+        if j == CHUNKS - 1:
+            again_from_above = again_from_row_neighbour(1)
+            start(again_from_above)
+        if j == CAP:
+            again_from_below = again_from_row_neighbour(-1)
+            start(again_from_below)
         if j in (0, 2):
             chain_stage(1 + j // 2)
     arrive(deeper)
@@ -304,6 +314,10 @@
     totals, groups = [], []
     for j in range(CHUNKS + 1):
         arrive(second[j])
+        if j == CHUNKS - 1:
+            arrive(again_from_below)
+        if j == CAP:
+            arrive(again_from_above)
         low, high = rows_at(B_ENDS, j, 3)
         step(f2, low, high, 5, store_to(fv))
         zero_sides(fv, low, high)

time: 36.6 us -> 34.8 us (0.951)
  Pallas kernels: 33 us -> 31.5 us
    pallas_call x1, Pallas kernels: 33 us -> 31.5 us  [body(): pl.pallas_call(kernel, out_shape=(jax.ShapeDtypeStruct((NY, NX, M), f32),...]
where the time goes in v4:
time: 34.8 us; the launch traced here: 34.6 us
  Pallas kernels  31.5 us (91%)
  other arithmetic  1.39 us (4%)
  local copies, waits for them, and re-layouts  1.14 us (3%)
  between operations  0.64 us (2%)
    pallas_call x1, Pallas kernels, body(): pl.pallas_call(kernel, out_shape=(jax.ShapeDtypeStruct((NY, NX, M), f32),...  31.5 us
    mul x1, other arithmetic, body(): potential = (here + below[:, None, :]) * (1.0 / 1024)  1.39 us
    unnamed x1, local copies, waits for them, and re-layouts  1.14 us

profile of v4, /device:TPU:104, one launch (start us, length us, event | category | flops | bytes accessed | tf_op | source)
XLA Modules:
  0.0 34.6 jit_solution(8121414430565320413)
XLA Ops:
  0.6 31.5 %shard_map.41 = (f32[96,32,128]{2,1,0:T(8,128)S(1)}, f32[96,32,128]{2,1,0:T(8,128)S(1)}, f32[96,128]{1,0:T(8,128)S(1)}) custom-call(f32[96,32,128]{2,1,0:T(8,128)} %tracer.1, f32[96,32,128]{2,1,0:T(8,128)} %crowding.1), custom_call_target="tpu_custom_call" | custom-call | tf_op jit(solution)/shard_map/pallas_call | solution.py:366
  32.1 1.4 %add_multiply_fusion = f32[96,32,128]{2,1,0:T(8,128)} fusion(f32[96,32,128]{2,1,0:T(8,128)S(1)} %get-tuple-element.5, f32[96,128]{1,0:T(8,128)S(1)} %get-tuple-element.6), kind=kLoop, calls=%fused_computation | loop fusion | flops 786432 | bytes 3194880 | tf_op jit(solution)/shard_map/mul | solution.py:392
  33.5 1.1 %copy.5 = f32[96,32,128]{2,1,0:T(8,128)} copy(f32[96,32,128]{2,1,0:T(8,128)S(1)} %get-tuple-element.11) | data formatting | bytes 3145728

commit v5 on v4

--- a/solution.py
+++ b/solution.py
@@ -19,7 +19,7 @@
 
 CHUNKS = 4
 CAP = CHUNKS
-A_ENDS = (37, 61, 85, NY + 2)
+A_ENDS = (37, 61, 85, NY + 3)
 B_ENDS = (36, 60, 84, NY + DY)
 MAIN = (0, 38, 62, 86, NY)
 COUNT = 96
@@ -27,7 +27,7 @@
 
 def kernel(
     tracer, crowding, end, here, below,
-    u, v, w, w_deep, t2, tot, p1, p2, group,
+    u, v, w, u2, t3, tot, p1, p2, group,
     in_sem, send_sems, recv_sems, chain,
 ):
     r = lax.axis_index("rows")
@@ -70,7 +70,7 @@
 
     is_left, is_right, is_top, is_bottom = c == 0, c == n_c - 1, r == 0, r == n_r - 1
     flat = lambda ref: ref.reshape(ROWS * PITCH, M)
-    fu, fv, fw, f2 = flat(u), flat(v), flat(w), flat(t2)
+    fu, fv, fw, fu2, f3 = flat(u), flat(v), flat(w), flat(u2), flat(t3)
 
     def zero_sides(f, low, high):
         zero = jnp.zeros((high + 1 - low, M), jnp.float32)
@@ -93,9 +93,9 @@
                     f[pl.ds((Y0 + row) * PITCH - 4, PITCH), :] = zero
 
     zero_sides(fu, -DY, NY + DY)
-    zero_sides(f2, -DY, NY + DY)
+    zero_sides(f3, -DY, NY + DY)
     zero_rows(fu, -DY, NY + DY)
-    zero_rows(f2, -DY, NY + DY)
+    zero_rows(f3, -DY, NY + DY)
 
     sent = []
     used = [0]
@@ -151,14 +151,14 @@
         return halo(ref, rows, edge_cols(dc, 0, depth) if dc else (0, NX), dr, dc)
 
     def from_row_neighbour(dr):
-        out = [row_halo(u, 0, 2, dr, 0), row_halo(w, 0, 1, dr, 0)]
+        out = [row_halo(u, 0, 3, dr, 0), row_halo(w, 0, 2, dr, 0)]
         for dc in (-1, 1):
-            out.append(row_halo(u, 0, 2, dr, dc, 2))
-            out.append(row_halo(w, 0, 3, dr, dc, 3))
+            out.append(row_halo(u, 0, 3, dr, dc, 3))
+            out.append(row_halo(w, 0, 2, dr, dc, 2))
         return out
 
     def again_from_row_neighbour(dr):
-        return [row_halo(t2, 0, 4, dr, dc, 4) for dc in (0, -1, 1)]
+        return [row_halo(t3, 0, 3, dr, dc, 3) for dc in (0, -1, 1)]
 
     from_below = from_row_neighbour(-1)
     from_above = from_row_neighbour(1)
@@ -166,21 +166,13 @@
     for j in range(CHUNKS):
         rows = (MAIN[j], MAIN[j + 1])
         first.append(
-            [halo(u, rows, edge_cols(dc, 0, 2), 0, dc) for dc in (-1, 1)]
-            + [halo(w, rows, edge_cols(dc, 0, 1), 0, dc) for dc in (-1, 1)]
+            [halo(u, rows, edge_cols(dc, 0, 3), 0, dc) for dc in (-1, 1)]
+            + [halo(w, rows, edge_cols(dc, 0, 2), 0, dc) for dc in (-1, 1)]
         )
-    deeper = [
-        (exists(0, dc), exists(0, -dc), copy_to(
-            w.at[Y0 : Y0 + NY, 1:3, :] if dc < 0 else w.at[Y0 : Y0 + NY, NX - 3 : NX - 1, :],
-            w_deep.at[Y0 : Y0 + NY, 1:3, :] if dc < 0 else w_deep.at[Y0 - 1 : Y0 + NY - 1, 5:7, :],
-            neighbour(0, dc),
-        ))
-        for dc in (-1, 1)
-    ] + [row_halo(w, 1, 3, dr, 0) for dr in (-1, 1)]
     start(from_above)
     start(from_below)
     start(first[0])
-    for items in first[1:] + [deeper]:
+    for items in first[1:]:
         start(items)
     first_sends = len(sent)
 
@@ -253,8 +245,12 @@
         zero_sides(fv, low, high)
         zero_rows(fv, low, high)
         low, high = rows_at(A_ENDS, j, 2)
-        step(fv, low, high, 4, store_to(f2))
-        items = [halo(t2, (low, high), edge_cols(dc, 0, 4), 0, dc) for dc in (-1, 1)]
+        step(fv, low, high, 5, store_to(fu2))
+        zero_sides(fu2, low, high)
+        zero_rows(fu2, low, high)
+        low, high = rows_at(A_ENDS, j, 3)
+        step(fu2, low, high, 4, store_to(f3))
+        items = [halo(t3, (low, high), edge_cols(dc, 0, 3), 0, dc) for dc in (-1, 1)]
         start(items)
         second.append(items)
         if j == CHUNKS - 1:
@@ -265,20 +261,8 @@
             start(again_from_below)
         if j in (0, 2):
             chain_stage(1 + j // 2)
-    arrive(deeper)
     finish(first_sends)
 
-    def merge(row, low, high):
-        mask = (place > low) & (place < high)
-        w[row, NX:PITCH, :] = jnp.where(mask, w_deep[row], w[row, NX:PITCH, :])
-
-    def merge_row(i, _):
-        merge(i, 0, 7)
-        return 0
-
-    merge(Y0 - 1, 4, 7)
-    lax.fori_loop(Y0, Y0 + NY - 1, merge_row, 0, unroll=5)
-    merge(Y0 + NY - 1, 0, 4)
 
     def store_end(row, base, new, first_row):
         for k, value in enumerate(new):
@@ -318,20 +302,16 @@
             arrive(again_from_below)
         if j == CAP:
             arrive(again_from_above)
-        low, high = rows_at(B_ENDS, j, 3)
-        step(f2, low, high, 5, store_to(fv))
+        low, high = rows_at(B_ENDS, j, 4)
+        step(f3, low, high, 5, store_to(fv))
         zero_sides(fv, low, high)
         zero_rows(fv, low, high)
-        low, high = rows_at(B_ENDS, j, 4)
+        low, high = rows_at(B_ENDS, j, 5)
         step(fv, low, high, 5, store_to(fu))
         zero_sides(fu, low, high)
         zero_rows(fu, low, high)
-        low, high = rows_at(B_ENDS, j, 5)
-        step(fu, low, high, 5, store_to(fv))
-        zero_sides(fv, low, high)
-        zero_rows(fv, low, high)
         low, high = rows_at(B_ENDS, j, 6)
-        step(fv, low, high, 4, functools.partial(store_end, first_row=low), last=True)
+        step(fu, low, high, 4, functools.partial(store_end, first_row=low), last=True)
         if j == CHUNKS - 1:
             continue
         k = min(j, CHUNKS - 1)
@@ -376,7 +356,7 @@
             pltpu.VMEM((ROWS, PITCH, M), f32),
             pltpu.VMEM((ROWS, PITCH, M), f32),
             pltpu.VMEM((ROWS, PITCH, M), f32),
-            pltpu.VMEM((ROWS, 8, M), f32),
+            pltpu.VMEM((ROWS, PITCH, M), f32),
             pltpu.VMEM((ROWS, PITCH, M), f32),
             pltpu.VMEM((NY, M), f32),
             pltpu.VMEM((4, NY, M), f32),

time: 34.8 us -> 33.5 us (0.963)
  Pallas kernels: 31.5 us -> 29.9 us
    pallas_call x1, Pallas kernels: 31.5 us -> 29.9 us  [body(): pl.pallas_call(kernel, out_shape=(jax.ShapeDtypeStruct((NY, NX, M), f32),...]
where the time goes in v5:
time: 33.5 us; the launch traced here: 33.1 us
  Pallas kernels  29.9 us (89%)
  other arithmetic  1.39 us (4%)
  local copies, waits for them, and re-layouts  1.14 us (3%)
  between operations  0.64 us (2%)
    pallas_call x1, Pallas kernels, body(): pl.pallas_call(kernel, out_shape=(jax.ShapeDtypeStruct((NY, NX, M), f32),...  29.9 us
    mul x1, other arithmetic, body(): potential = (here + below[:, None, :]) * (1.0 / 1024)  1.39 us
    unnamed x1, local copies, waits for them, and re-layouts  1.14 us

profile of v5, /device:TPU:104, one launch (start us, length us, event | category | flops | bytes accessed | tf_op | source)
XLA Modules:
  0.0 33.1 jit_solution(11150950196787005669)
XLA Ops:
  0.6 29.9 %shard_map.41 = (f32[96,32,128]{2,1,0:T(8,128)S(1)}, f32[96,32,128]{2,1,0:T(8,128)S(1)}, f32[96,128]{1,0:T(8,128)S(1)}) custom-call(f32[96,32,128]{2,1,0:T(8,128)} %tracer.1, f32[96,32,128]{2,1,0:T(8,128)} %crowding.1), custom_call_target="tpu_custom_call" | custom-call | tf_op jit(solution)/shard_map/pallas_call | solution.py:346
  30.6 1.4 %add_multiply_fusion = f32[96,32,128]{2,1,0:T(8,128)} fusion(f32[96,32,128]{2,1,0:T(8,128)S(1)} %get-tuple-element.5, f32[96,128]{1,0:T(8,128)S(1)} %get-tuple-element.6), kind=kLoop, calls=%fused_computation | loop fusion | flops 786432 | bytes 3194880 | tf_op jit(solution)/shard_map/mul | solution.py:372
  32.0 1.1 %copy.5 = f32[96,32,128]{2,1,0:T(8,128)} copy(f32[96,32,128]{2,1,0:T(8,128)S(1)} %get-tuple-element.11) | data formatting | bytes 3145728

commit v6 on v5

--- a/solution.py
+++ b/solution.py
@@ -338,6 +338,30 @@
             below[0:DY, :] = before[NY - at :]
     finish()
 
+PIECES = 4
+
+
+def write_out(here, below, end, potential_out, end_out, potential, sems):
+    rest = pltpu.make_async_copy(end, end_out, sems.at[PIECES])
+    rest.start()
+    rows = NY // PIECES
+    pieces = []
+    for k in range(PIECES):
+        part = slice(k * rows, (k + 1) * rows)
+
+        def row(i, _):
+            potential[i] = (here[i] + below[pl.ds(i, 1), :]) * (1.0 / 1024)
+            return 0
+
+        lax.fori_loop(k * rows, (k + 1) * rows, row, 0, unroll=4)
+        piece = pltpu.make_async_copy(potential.at[part], potential_out.at[part], sems.at[k])
+        piece.start()
+        pieces.append(piece)
+    for piece in pieces:
+        piece.wait()
+    rest.wait()
+
+
 def body(tracer, crowding):
     vmem = pl.BlockSpec(memory_space=pltpu.VMEM)
     hbm = pl.BlockSpec(memory_space=pltpu.HBM)
@@ -369,7 +393,14 @@
             collective_id=0, has_side_effects=True, vmem_limit_bytes=50 * 1024 * 1024
         ),
     )(tracer, crowding)
-    potential = (here + below[:, None, :]) * (1.0 / 1024)
+    potential, end = pl.pallas_call(
+        write_out,
+        out_shape=(jax.ShapeDtypeStruct((NY, NX, M), f32), jax.ShapeDtypeStruct((NY, NX, M), f32)),
+        in_specs=[vmem, vmem, vmem],
+        out_specs=(hbm, hbm),
+        scratch_shapes=[pltpu.VMEM((NY, NX, M), f32), dma((PIECES + 1,))],
+        compiler_params=pltpu.CompilerParams(vmem_limit_bytes=8 * 1024 * 1024),
+    )(here, below, end)
     return (potential, end)
 
 

time: 33.5 us -> 32.7 us (0.976)
  Pallas kernels: 29.9 us -> 31.6 us
  other arithmetic: 1.39 us -> 0 us
  local copies, waits for them, and re-layouts: 1.14 us -> 0 us
    pallas_call x0 -> x1, Pallas kernels: none -> 1.7 us  [body(): pl.pallas_call(write_out, out_shape=(jax.ShapeDtypeStruct((NY, NX, M), f3...]
    mul x1 -> x0, other arithmetic: 1.39 us -> none  [body(): potential = (here + below[:, None, :]) * (1.0 / 1024)]
    unnamed x1 -> x0, local copies, waits for them, and re-layouts: 1.14 us -> none
where the time goes in v6:
time: 32.7 us; the launch traced here: 32.3 us
  Pallas kernels  31.6 us (97%)
  between operations  0.64 us (2%)
    pallas_call x1, Pallas kernels, body(): pl.pallas_call(kernel, out_shape=(jax.ShapeDtypeStruct((NY, NX, M), f32),...  29.9 us
    pallas_call x1, Pallas kernels, body(): pl.pallas_call(write_out, out_shape=(jax.ShapeDtypeStruct((NY, NX, M), f3...  1.7 us

profile of v6, /device:TPU:104, one launch (start us, length us, event | category | flops | bytes accessed | tf_op | source)
XLA Modules:
  0.0 32.3 jit_solution(7868290093462822015)
XLA Ops:
  0.6 29.9 %shard_map.41 = (f32[96,32,128]{2,1,0:T(8,128)S(1)}, f32[96,32,128]{2,1,0:T(8,128)S(1)}, f32[96,128]{1,0:T(8,128)S(1)}) custom-call(f32[96,32,128]{2,1,0:T(8,128)} %tracer.1, f32[96,32,128]{2,1,0:T(8,128)} %crowding.1), custom_call_target="tpu_custom_call" | custom-call | tf_op jit(solution)/shard_map/pallas_call | solution.py:370
  30.6 1.7 %shard_map.42 = (f32[96,32,128]{2,1,0:T(8,128)}, f32[96,32,128]{2,1,0:T(8,128)}) custom-call(f32[96,32,128]{2,1,0:T(8,128)S(1)} %get-tuple-element.5.here, f32[96,128]{1,0:T(8,128)S(1)} %get-tuple-element.6.below, f32[96,32,128]{2,1,0:T(8,128)S(1)} %get-tuple-element.7.end), custom_call_target="tpu_custom_call" | custom-call | tf_op jit(solution)/shard_map/pallas_call | solution.py:396

commit v7 on v6

--- a/solution.py
+++ b/solution.py
@@ -216,7 +216,7 @@
         at = (Y0 + low - 1) * PITCH
         north = tuple(src[pl.ds(at + 8 * k, 8), :] for k in range(tiles))
         centre = tuple(src[pl.ds(at + PITCH + 8 * k, 8), :] for k in range(tiles))
-        lax.fori_loop(0, high - low, body, (north, centre), unroll=2)
+        lax.fori_loop(0, high - low, body, (north, centre), unroll=4 if high - low > 8 else high - low)
 
     def store_to(dst):
         def store(row, base, new):

time: 32.7 us -> 32.3 us (0.988)
  Pallas kernels: 31.6 us -> 31.2 us
    pallas_call x1, Pallas kernels: 29.9 us -> 29.5 us  [body(): pl.pallas_call(kernel, out_shape=(jax.ShapeDtypeStruct((NY, NX, M), f32),...]
where the time goes in v7:
time: 32.3 us; the launch traced here: 31.9 us
  Pallas kernels  31.2 us (97%)
  between operations  0.64 us (2%)
    pallas_call x1, Pallas kernels, body(): pl.pallas_call(kernel, out_shape=(jax.ShapeDtypeStruct((NY, NX, M), f32),...  29.5 us
    pallas_call x1, Pallas kernels, body(): pl.pallas_call(write_out, out_shape=(jax.ShapeDtypeStruct((NY, NX, M), f3...  1.7 us

profile of v7, /device:TPU:104, one launch (start us, length us, event | category | flops | bytes accessed | tf_op | source)
XLA Modules:
  0.0 31.9 jit_solution(2811435318141256555)
XLA Ops:
  0.6 29.5 %shard_map.41 = (f32[96,32,128]{2,1,0:T(8,128)S(1)}, f32[96,32,128]{2,1,0:T(8,128)S(1)}, f32[96,128]{1,0:T(8,128)S(1)}) custom-call(f32[96,32,128]{2,1,0:T(8,128)} %tracer.1, f32[96,32,128]{2,1,0:T(8,128)} %crowding.1), custom_call_target="tpu_custom_call" | custom-call | tf_op jit(solution)/shard_map/pallas_call | solution.py:370
  30.2 1.7 %shard_map.42 = (f32[96,32,128]{2,1,0:T(8,128)}, f32[96,32,128]{2,1,0:T(8,128)}) custom-call(f32[96,32,128]{2,1,0:T(8,128)S(1)} %get-tuple-element.5.here, f32[96,128]{1,0:T(8,128)S(1)} %get-tuple-element.6.below, f32[96,32,128]{2,1,0:T(8,128)S(1)} %get-tuple-element.7.end), custom_call_target="tpu_custom_call" | custom-call | tf_op jit(solution)/shard_map/pallas_call | solution.py:396

commit v8 on v7

--- a/solution.py
+++ b/solution.py
@@ -92,8 +92,8 @@
                 def _(row=row):
                     f[pl.ds((Y0 + row) * PITCH - 4, PITCH), :] = zero
 
-    zero_sides(fu, -DY, NY + DY)
-    zero_sides(f3, -DY, NY + DY)
+    zero_sides(fu, -4, NY + 3)
+    zero_sides(f3, -4, NY + 3)
     zero_rows(fu, -DY, NY + DY)
     zero_rows(f3, -DY, NY + DY)
 
@@ -372,7 +372,7 @@
         out_shape=(
             jax.ShapeDtypeStruct((NY, NX, M), f32),
             jax.ShapeDtypeStruct((NY, NX, M), f32),
-            jax.ShapeDtypeStruct((NY, M), f32),
+            jax.ShapeDtypeStruct((NY + 8, M), f32),
         ),
         in_specs=[hbm, hbm],
         out_specs=(vmem, vmem, vmem),
@@ -382,7 +382,7 @@
             pltpu.VMEM((ROWS, PITCH, M), f32),
             pltpu.VMEM((ROWS, PITCH, M), f32),
             pltpu.VMEM((ROWS, PITCH, M), f32),
-            pltpu.VMEM((NY, M), f32),
+            pltpu.VMEM((NY + 8, M), f32),
             pltpu.VMEM((4, NY, M), f32),
             pltpu.VMEM((8, NY, M), f32),
             pltpu.VMEM((NY, M), f32),

time: 32.3 us -> 32.3 us (level)
  no operation moved by 1% of the time
where the time goes in v8:
time: 32.3 us; the launch traced here: 31.9 us
  Pallas kernels  31.2 us (97%)
  between operations  0.64 us (2%)
    pallas_call x1, Pallas kernels, body(): pl.pallas_call(kernel, out_shape=(jax.ShapeDtypeStruct((NY, NX, M), f32),...  29.5 us
    pallas_call x1, Pallas kernels, body(): pl.pallas_call(write_out, out_shape=(jax.ShapeDtypeStruct((NY, NX, M), f3...  1.7 us

profile of v8, /device:TPU:104, one launch (start us, length us, event | category | flops | bytes accessed | tf_op | source)
XLA Modules:
  0.0 31.9 jit_solution(12313354911135478531)
XLA Ops:
  0.6 29.5 %shard_map.41 = (f32[96,32,128]{2,1,0:T(8,128)S(1)}, f32[96,32,128]{2,1,0:T(8,128)S(1)}, f32[104,128]{1,0:T(8,128)S(1)}) custom-call(f32[96,32,128]{2,1,0:T(8,128)} %tracer.1, f32[96,32,128]{2,1,0:T(8,128)} %crowding.1), custom_call_target="tpu_custom_call" | custom-call | tf_op jit(solution)/shard_map/pallas_call | solution.py:370
  30.2 1.7 %shard_map.42 = (f32[96,32,128]{2,1,0:T(8,128)}, f32[96,32,128]{2,1,0:T(8,128)}) custom-call(f32[96,32,128]{2,1,0:T(8,128)S(1)} %get-tuple-element.5.here, f32[104,128]{1,0:T(8,128)S(1)} %get-tuple-element.6.below, f32[96,32,128]{2,1,0:T(8,128)S(1)} %get-tuple-element.7.end), custom_call_target="tpu_custom_call" | custom-call | tf_op jit(solution)/shard_map/pallas_call | solution.py:396

commit v9 on v8

--- a/solution.py
+++ b/solution.py
@@ -216,7 +216,7 @@
         at = (Y0 + low - 1) * PITCH
         north = tuple(src[pl.ds(at + 8 * k, 8), :] for k in range(tiles))
         centre = tuple(src[pl.ds(at + PITCH + 8 * k, 8), :] for k in range(tiles))
-        lax.fori_loop(0, high - low, body, (north, centre), unroll=4 if high - low > 8 else high - low)
+        lax.fori_loop(0, high - low, body, (north, centre), unroll=6 if high - low > 14 else high - low)
 
     def store_to(dst):
         def store(row, base, new):

time: 32.3 us -> 32.2 us (level)
  no operation moved by 1% of the time
where the time goes in v9:
time: 32.2 us; the launch traced here: 31.6 us
  Pallas kernels  30.9 us (96%)
  between operations  0.64 us (2%)
    pallas_call x1, Pallas kernels, body(): pl.pallas_call(kernel, out_shape=(jax.ShapeDtypeStruct((NY, NX, M), f32),...  29.2 us
    pallas_call x1, Pallas kernels, body(): pl.pallas_call(write_out, out_shape=(jax.ShapeDtypeStruct((NY, NX, M), f3...  1.7 us

profile of v9, /device:TPU:104, one launch (start us, length us, event | category | flops | bytes accessed | tf_op | source)
XLA Modules:
  0.0 31.6 jit_solution(11545718737850104419)
XLA Ops:
  0.6 29.2 %shard_map.41 = (f32[96,32,128]{2,1,0:T(8,128)S(1)}, f32[96,32,128]{2,1,0:T(8,128)S(1)}, f32[104,128]{1,0:T(8,128)S(1)}) custom-call(f32[96,32,128]{2,1,0:T(8,128)} %tracer.1, f32[96,32,128]{2,1,0:T(8,128)} %crowding.1), custom_call_target="tpu_custom_call" | custom-call | tf_op jit(solution)/shard_map/pallas_call | solution.py:370
  29.9 1.7 %shard_map.42 = (f32[96,32,128]{2,1,0:T(8,128)}, f32[96,32,128]{2,1,0:T(8,128)}) custom-call(f32[96,32,128]{2,1,0:T(8,128)S(1)} %get-tuple-element.5.here, f32[104,128]{1,0:T(8,128)S(1)} %get-tuple-element.6.below, f32[96,32,128]{2,1,0:T(8,128)S(1)} %get-tuple-element.7.end), custom_call_target="tpu_custom_call" | custom-call | tf_op jit(solution)/shard_map/pallas_call | solution.py:396
